TPU v7x, 32 devices: a whole 2x2x4 slice. The times are simulated.
32 devices in a mesh: row: 8 (over z, y), col: 4 (over x, core).
Axes of the slice: x: 2, y: 2, z: 4, core: 2. Of those that a mesh axis runs over, the one named last changes fastest.
Arguments:
- matrix: bfloat16 [32768, 32768], P('row', 'col'), may hold values from -0.03125 to 0.03125
- right_sides: float32 [32768, 64], P(('row', 'col')), may hold values from -6 to 6
- initial_guess: float32 [32768, 64], P(('row', 'col')), may hold values from -6 to 6
Outputs:
- solution: float32 [32768, 64], P(('row', 'col'))
All inputs are finite; a program needn't handle non-finite values.
Results may differ from a plain program's by a relative error of at most 0.0038.
Values may be sent and summed in bfloat16 or wider, within the bound.
A program may use at most 128 MiB of HBM per device.

v0:
```python
import jax
import jax.numpy as jnp
from jax import lax
from jax.sharding import PartitionSpec as P

STEPS = 3
DIAGONAL_SHIFT = 1.4


def inner_products(left, right):
    return jnp.einsum("rk,rs->ks", left, right, precision=lax.Precision.HIGHEST)


def combine_basis(stacked, weights):
    return jnp.dot(stacked, weights, precision=lax.Precision.HIGHEST)


def orthonormal(applied, gram_sum):
    lower_factor = jnp.linalg.cholesky(gram_sum)
    basis_next = lax.linalg.triangular_solve(
        lower_factor, applied, left_side=False, lower=True, transpose_a=True
    )
    return (basis_next, lower_factor.T)


def least_squares(column_list, top_factor):
    span_width = top_factor.shape[0]
    count = len(column_list)
    pieces = []
    for position, (projected, upper_factor) in enumerate(column_list):
        filler = jnp.zeros(((count - position - 1) * span_width, span_width), jnp.float32)
        pieces.append(jnp.concatenate([projected, upper_factor, filler], axis=0))
    hessenberg = jnp.concatenate(pieces, axis=1)
    normal_matrix = inner_products(hessenberg, hessenberg)
    target = inner_products(hessenberg[:span_width], top_factor)
    lower_factor = jnp.linalg.cholesky(normal_matrix)
    halfway = lax.linalg.triangular_solve(lower_factor, target, left_side=True, lower=True)
    return lax.linalg.triangular_solve(
        lower_factor, halfway, left_side=True, lower=True, transpose_a=True
    )


def per_device(matrix, right_sides, initial_guess):

    def fold_panel(panel_piece):
        return jnp.dot(matrix, panel_piece, preferred_element_type=jnp.float32)

    def operate(local_block):
        operand = local_block.astype(jnp.bfloat16)
        partial_sum = fold_panel(lax.all_gather(operand, "row", axis=0, tiled=True))
        product = lax.psum_scatter(partial_sum, "col", scatter_dimension=0, tiled=True)
        return DIAGONAL_SHIFT * local_block + product

    def reduce_all(local_sum):
        return lax.psum(local_sum, ("row", "col"))

    guess_local, sides_local = (initial_guess, right_sides)
    residual_start = sides_local - operate(guess_local)
    basis_now, top_factor = orthonormal(
        residual_start, reduce_all(inner_products(residual_start, residual_start))
    )
    basis_list = [basis_now]
    column_list = []
    for iteration in range(STEPS):
        applied = operate(basis_list[-1])
        stacked = jnp.concatenate(basis_list, axis=1)
        span_width = stacked.shape[1]
        combined = reduce_all(inner_products(jnp.concatenate([stacked, applied], axis=1), applied))
        projected = combined[:span_width]
        gram_sum = combined[span_width:] - inner_products(projected, projected)
        applied = applied - combine_basis(stacked, projected)
        basis_now, upper_factor = orthonormal(applied, gram_sum)
        basis_list.append(basis_now)
        column_list.append((projected, upper_factor))
    coefficients = least_squares(column_list, top_factor)
    update = combine_basis(jnp.concatenate(basis_list[:-1], axis=1), coefficients)
    return guess_local + update


def solution(mesh):
    return jax.shard_map(
        per_device,
        mesh=mesh,
        in_specs=(P("row", "col"), P(("row", "col"), None), P(("row", "col"), None)),
        out_specs=P(("row", "col"), None),
        check_vma=False,
    )
```

profile of v0, /device:TPU:1, one launch (start us, length us, event | category | flops | bytes accessed | tf_op | source)
XLA Modules:
  0.0 751.0 jit_solution(7809911143641430685)
XLA Ops:
  6.5 1.7 convert_element_type.12
  8.3 41.9 %all-gather.5.cloned.1.call-done = bf16[8192,64]{0,1:T(8,128)(2,1)} async-done(((bf16[1024,64]{0,1:T(8,128)(2,1)}), bf16[8192,64]{0,1:T(8,128)(2,1)}) %all-gather.5.cloned.1.call-update) | async-done | bytes 1048592 | tf_op jit(solution)/shard_map/all_gather | solution.py:50
  50.2 29.6 %fusion.97 = f32[4096,64]{0,1:T(8,128)} fusion(bf16[4096,8192]{1,0:T(8,128)(2,1)} %param.6, bf16[8192,64]{0,1:T(8,128)(2,1)} %all-gather.5.cloned.1.call-done), kind=kOutput, calls=%fused_computation.157 | convolution fusion | flops 4294967296 | bytes 69206016 | tf_op jit(solution)/shard_map/dot_general | solution.py:46
  79.9 25.2 %reduce-scatter.5.cloned.1.call-done = f32[1024,64]{0,1:T(8,128)} async-done(((f32[4096,64]{0,1:T(8,128)}), f32[1024,64]{0,1:T(8,128)}) %reduce-scatter.5.cloned.1.call-update) | async-done | bytes 262160 | tf_op jit(solution)/shard_map/reduce_scatter | solution.py:51
  105.0 1.4 fusion.93
  106.5 38.8 %psum.28 = f32[64,64]{0,1:T(8,128)S(1)} all-reduce(f32[64,64]{0,1:T(8,128)S(1)} %fusion.93), channel_id=1, replica_groups=mesh['row'=8,'col'=4] {'row','col'}, use_global_device_ids=true, to_apply=%region_1.0 | all-reduce | flops 4096 | bytes 32768 | tf_op jit(solution)/shard_map/psum | solution.py:55
  145.4 5.8 cholesky.195
  151.3 0.7 compare_reduce_fusion.3
  152.0 0.6 select_bitcast_fusion.4
  152.6 4.9 custom-call.25
  157.5 2.0 fusion.94
  159.6 40.1 %all-gather.7.cloned.1.call-done = bf16[8192,64]{0,1:T(8,128)(2,1)} async-done(((bf16[1024,64]{0,1:T(8,128)(2,1)}), bf16[8192,64]{0,1:T(8,128)(2,1)}) %all-gather.7.cloned.1.call-update) | async-done | bytes 1048592 | tf_op jit(solution)/shard_map/all_gather | solution.py:50
  199.7 28.4 %convolution_bitcast_fusion.2 = f32[4096,64]{0,1:T(8,128)} fusion(bf16[8192,64]{0,1:T(8,128)(2,1)} %all-gather.7.cloned.1.call-done, bf16[4096,8192]{1,0:T(8,128)(2,1)} %param.6), kind=kOutput, calls=%fused_computation.2 | convolution fusion | flops 4294967296 | bytes 69206016 | tf_op jit(solution)/shard_map/dot_general | solution.py:46
  228.2 25.1 %reduce-scatter.7.cloned.1.call-done = f32[1024,64]{0,1:T(8,128)} async-done(((f32[4096,64]{0,1:T(8,128)}), f32[1024,64]{0,1:T(8,128)}) %reduce-scatter.7.cloned.1.call-update) | async-done | bytes 262160 | tf_op jit(solution)/shard_map/reduce_scatter | solution.py:51
  253.4 1.0 multiply_add_fusion.2
  254.3 0.7 fusion.13
  255.0 39.0 %psum.29 = f32[128,64]{0,1:T(8,128)S(1)} all-reduce(f32[128,64]{0,1:T(8,128)S(1)} %fusion.13), channel_id=1, replica_groups=mesh['row'=8,'col'=4] {'row','col'}, use_global_device_ids=true, to_apply=%region_5.8 | all-reduce | flops 8192 | bytes 65536 | tf_op jit(solution)/shard_map/psum | solution.py:55
  294.1 0.2 convolution_subtract_fusion.7
  294.3 5.8 cholesky.206
  300.2 0.6 compare_reduce_fusion.2
  300.9 0.7 fusion.74
  301.5 4.9 custom-call.26
  306.4 1.3 convolution_subtract_fusion.1
  307.8 1.1 fusion.95
  308.9 40.2 %all-gather.9.cloned.1.call-done = bf16[8192,64]{0,1:T(8,128)(2,1)} async-done(((bf16[1024,64]{0,1:T(8,128)(2,1)}), bf16[8192,64]{0,1:T(8,128)(2,1)}) %all-gather.9.cloned.1.call-update) | async-done | bytes 1048592 | tf_op jit(solution)/shard_map/all_gather | solution.py:50
  349.1 28.4 %convolution_bitcast_fusion.1 = f32[4096,64]{0,1:T(8,128)} fusion(bf16[8192,64]{0,1:T(8,128)(2,1)} %all-gather.9.cloned.1.call-done, bf16[4096,8192]{1,0:T(8,128)(2,1)} %param.6), kind=kOutput, calls=%fused_computation.1 | convolution fusion | flops 4294967296 | bytes 69206016 | tf_op jit(solution)/shard_map/dot_general | solution.py:46
  377.6 25.2 %reduce-scatter.9.cloned.1.call-done = f32[1024,64]{0,1:T(8,128)} async-done(((f32[4096,64]{0,1:T(8,128)}), f32[1024,64]{0,1:T(8,128)}) %reduce-scatter.9.cloned.1.call-update) | async-done | bytes 262160 | tf_op jit(solution)/shard_map/reduce_scatter | solution.py:51
  402.7 1.0 multiply_add_fusion.1
  403.7 0.9 fusion.8
  404.6 39.0 %psum.30 = f32[192,64]{0,1:T(8,128)S(1)} all-reduce(f32[192,64]{0,1:T(8,128)S(1)} %fusion.8), channel_id=1, replica_groups=mesh['row'=8,'col'=4] {'row','col'}, use_global_device_ids=true, to_apply=%region_7.10 | all-reduce | flops 12288 | bytes 98304 | tf_op jit(solution)/shard_map/psum | solution.py:55
  443.6 0.2 convolution_subtract_fusion.6
  443.8 5.8 cholesky.217
  449.7 0.6 compare_reduce_fusion.1
  450.4 0.7 fusion.75
  451.0 4.9 custom-call.27
  455.9 1.4 convolution_subtract_fusion
  457.3 1.1 fusion.96
  458.5 40.2 %all-gather.11.cloned.1.call-done = bf16[8192,64]{0,1:T(8,128)(2,1)} async-done(((bf16[1024,64]{0,1:T(8,128)(2,1)}), bf16[8192,64]{0,1:T(8,128)(2,1)}) %all-gather.11.cloned.1.call-update) | async-done | bytes 1048592 | tf_op jit(solution)/shard_map/all_gather | solution.py:50
  498.7 28.4 %convolution_bitcast_fusion = f32[4096,64]{0,1:T(8,128)} fusion(bf16[8192,64]{0,1:T(8,128)(2,1)} %all-gather.11.cloned.1.call-done, bf16[4096,8192]{1,0:T(8,128)(2,1)} %param.6), kind=kOutput, calls=%fused_computation | convolution fusion | flops 4294967296 | bytes 69206016 | tf_op jit(solution)/shard_map/dot_general | solution.py:46
  527.1 0.3 all-reduce.5.cloned.1.call-start
  527.4 24.9 %reduce-scatter.11.cloned.1.call-done = f32[1024,64]{0,1:T(8,128)} async-done(((f32[4096,64]{0,1:T(8,128)}), f32[1024,64]{0,1:T(8,128)}) %reduce-scatter.11.cloned.1.call-update) | async-done | bytes 262160 | tf_op jit(solution)/shard_map/reduce_scatter | solution.py:51
  552.3 1.0 multiply_add_fusion
  553.3 1.7 fusion
  555.1 124.3 %all-reduce.5.cloned.1.call-done = f32[256,64]{0,1:T(8,128)} async-done(((f32[256,64]{0,1:T(8,128)}), f32[256,64]{0,1:T(8,128)}) %all-reduce.5.cloned.1.call-update) | async-done | bytes 65552 | tf_op jit(solution)/shard_map/psum | solution.py:55
  679.4 1.1 convolution_subtract_fusion.5
  680.6 5.8 cholesky.228
  686.5 0.6 compare_reduce_fusion
  687.1 0.7 select_bitcast_fusion.1
  687.8 1.3 fusion.16
  689.3 11.7 %cholesky.77 = f32[128,128]{1,0:T(8,128)S(1)} custom-call(f32[128,128]{1,0:T(8,128)S(1)} %cholesky.237), custom_call_target="Cholesky" | custom-call | tf_op jit(solution)/shard_map/jit(cholesky)/cholesky | solution.py:36
  701.1 1.8 fusion.33
  702.9 9.8 %custom-call.21 = f32[1,128,128]{1,2,0:T(8,128)S(1)} custom-call(f32[1,128,128]{2,1,0:T(8,128)S(1)} %get-tuple-element.28), custom_call_target="InvertDiagBlocksLowerTriangular" | custom-call | tf_op jit(solution)/shard_map/jit(cholesky)/cholesky | solution.py:36
  712.7 0.2 constant_dynamic-update-slice_fusion.1
  712.9 0.2 convolution_subtract_fusion.4
  713.1 5.8 cholesky.135
  718.9 0.6 compare_reduce_fusion.5
  719.6 0.7 compare_reduce_fusion.4
  721.8 19.9 %custom-call.22 = f32[2,128,128]{1,2,0:T(8,128)S(1)} custom-call(f32[2,128,128]{2,1,0:T(8,128)S(1)} %pad_maximum_fusion.7), custom_call_target="InvertDiagBlocksLowerTriangular" | custom-call | tf_op jit(solution)/shard_map/triangular_solve | solution.py:38
  741.8 0.2 fusion.56
  742.0 0.2 convolution_subtract_fusion.3
  742.1 0.2 fusion.70
  742.4 0.2 fusion.69
  742.9 0.2 fusion.55
  743.1 1.4 convolution_add_fusion
  (50 shorter events, 1.5 us)
Async XLA Ops:
  6.5 98.5 %copy-start = (f32[1024,64]{0,1:T(8,128)S(1)}, f32[1024,64]{0,1:T(8,128)}, u32[]{:S(2)}) copy-start(f32[1024,64]{0,1:T(8,128)} %param.8) | copy-start | bytes 786436
  6.5 98.5 %copy-start.1 = (f32[1024,64]{0,1:T(8,128)S(1)}, f32[1024,64]{0,1:T(8,128)}, u32[]{:S(2)}) copy-start(f32[1024,64]{0,1:T(8,128)} %param.7) | copy-start | bytes 786436
  6.5 43.6 %all-gather.5.cloned.1.call-start = ((), (), s32[]{:S(2)}) async-start(), calls=%async_computation.4 | async-start | bytes 1179648 | tf_op jit(solution)/shard_map/all_gather | solution.py:50
  8.3 96.8 %reduce-scatter.5.cloned.1.call-start = ((), (), s32[]{:S(2)}) async-start(), calls=%async_computation.5 | async-start | bytes 1310720 | tf_op jit(solution)/shard_map/reduce_scatter | solution.py:51
  79.8 119.9 %all-gather.7.cloned.1.call-start = ((), (), s32[]{:S(2)}) async-start(), calls=%async_computation.6 | async-start | bytes 1179648 | tf_op jit(solution)/shard_map/all_gather | solution.py:50
  159.6 93.8 %reduce-scatter.7.cloned.1.call-start = ((), (), s32[]{:S(2)}) async-start(), calls=%async_computation.7 | async-start | bytes 1310720 | tf_op jit(solution)/shard_map/reduce_scatter | solution.py:51
  228.2 121.0 %all-gather.9.cloned.1.call-start = ((), (), s32[]{:S(2)}) async-start(), calls=%async_computation.8 | async-start | bytes 1179648 | tf_op jit(solution)/shard_map/all_gather | solution.py:50
  308.9 93.9 %reduce-scatter.9.cloned.1.call-start = ((), (), s32[]{:S(2)}) async-start(), calls=%async_computation.9 | async-start | bytes 1310720 | tf_op jit(solution)/shard_map/reduce_scatter | solution.py:51
  377.5 121.2 %all-gather.11.cloned.1.call-start = ((), (), s32[]{:S(2)}) async-start(), calls=%async_computation.10 | async-start | bytes 1179648 | tf_op jit(solution)/shard_map/all_gather | solution.py:50
  458.4 93.9 %reduce-scatter.11.cloned.1.call-start = ((), (), s32[]{:S(2)}) async-start(), calls=%async_computation.11 | async-start | bytes 1310720 | tf_op jit(solution)/shard_map/reduce_scatter | solution.py:51
  527.1 152.3 %all-reduce.5.cloned.1.call-start = ((), (), s32[]{:S(2)}) async-start(), calls=%async_computation.12 | async-start | bytes 131072 | tf_op jit(solution)/shard_map/psum | solution.py:55
Sparse Core Ops, SparseCore 0:
  9.5 40.6 all-gather.4
  79.9 25.0 reduce-scatter.4
  159.7 40.0 all-gather.6
  228.3 25.0 reduce-scatter.6
  309.0 40.0 all-gather.8
  377.6 25.0 reduce-scatter.8
  458.5 40.1 all-gather.10
  527.2 25.0 reduce-scatter.10
  557.9 121.4 all-reduce.4
where the time goes:
time: 752 us; the launch traced here: 751 us
  waiting for transfers between devices  387 us (51%)
  matrix products  134 us (18%)
  blocking collectives  117 us (16%)
  other arithmetic  96.9 us (13%)
  between operations  14.9 us (2%)
    all_gather x4, waiting for transfers between devices, operate(): partial_sum = fold_panel(lax.all_gather(operand, 'row', axis=0, tiled=True))  162 us
    psum x1, waiting for transfers between devices, reduce_all(): return lax.psum(local_sum, ('row', 'col'))  124 us
    psum x3, blocking collectives, reduce_all(): return lax.psum(local_sum, ('row', 'col'))  117 us
    dot_general x4, matrix products, fold_panel(): return jnp.dot(matrix, panel_piece, preferred_element_type=jnp.float32)  115 us
    reduce_scatter x4, waiting for transfers between devices, operate(): lax.psum_scatter(partial_sum, 'col', scatter_dimension=0, tiled=True)  100 us
    another operation x7, other arithmetic, least_squares(): lower_factor = jnp.linalg.cholesky(normal_matrix)  28.8 us
    another operation x12, other arithmetic, orthonormal(): lower_factor = jnp.linalg.cholesky(gram_sum)  26.1 us
    another operation x6, other arithmetic, least_squares(): lax.linalg.triangular_solve(lower_factor, halfway, left_side=True, lower=...  20.1 us
  transfers between devices with their start and end apart: 9, of which 9 were waited for; matrix products, arithmetic and copies ran while one was open for 0% of the time, Pallas kernels for 0%

commit v1 on v0

--- a/solution.py
+++ b/solution.py
@@ -5,6 +5,12 @@
 
 STEPS = 3
 DIAGONAL_SHIFT = 1.4
+
+
+def add_all(x, mesh_axis):
+    parts = lax.all_gather(x, mesh_axis, axis=0, tiled=False)
+    summed = parts.sum(axis=0)
+    return summed
 
 
 def inner_products(left, right):
@@ -52,7 +58,7 @@
         return DIAGONAL_SHIFT * local_block + product
 
     def reduce_all(local_sum):
-        return lax.psum(local_sum, ("row", "col"))
+        return add_all(local_sum, ("row", "col"))
 
     guess_local, sides_local = (initial_guess, right_sides)
     residual_start = sides_local - operate(guess_local)

time: 752 us -> 714 us (0.949)
  blocking collectives: 117 us -> 44.2 us
  waiting for transfers between devices: 387 us -> 418 us
    all_gather x0 -> x3, waiting for transfers between devices: none -> 166 us  [add_all(): parts = lax.all_gather(x, mesh_axis, axis=0, tiled=False)]
    psum x1 -> x0, waiting for transfers between devices: 124 us -> none  [reduce_all(): return lax.psum(local_sum, ('row', 'col'))]
    psum x3 -> x0, blocking collectives: 117 us -> none  [reduce_all(): return lax.psum(local_sum, ('row', 'col'))]
    all_gather x0 -> x1, blocking collectives: none -> 44.2 us  [add_all(): parts = lax.all_gather(x, mesh_axis, axis=0, tiled=False)]
    all_gather x4, waiting for transfers between devices: 162 us -> 151 us  [operate(): partial_sum = fold_panel(lax.all_gather(operand, 'row', axis=0, tiled=True))]
  transfers between devices with their start and end apart: 9 -> 11, of which waited for: 9 -> 11; matrix products, arithmetic and copies ran while one was open for 0% -> 0% of each run, Pallas kernels for 0% -> 0%
where the time goes in v1:
time: 714 us; the launch traced here: 713 us
  waiting for transfers between devices  418 us (59%)
  matrix products  132 us (18%)
  other arithmetic  99 us (14%)
  blocking collectives  44.2 us (6%)
  between operations  14.9 us (2%)
    all_gather x3, waiting for transfers between devices, add_all(): parts = lax.all_gather(x, mesh_axis, axis=0, tiled=False)  166 us
    all_gather x4, waiting for transfers between devices, operate(): partial_sum = fold_panel(lax.all_gather(operand, 'row', axis=0, tiled=True))  151 us
    dot_general x4, matrix products, fold_panel(): return jnp.dot(matrix, panel_piece, preferred_element_type=jnp.float32)  115 us
    reduce_scatter x4, waiting for transfers between devices, operate(): lax.psum_scatter(partial_sum, 'col', scatter_dimension=0, tiled=True)  100 us
    all_gather x1, blocking collectives, add_all(): parts = lax.all_gather(x, mesh_axis, axis=0, tiled=False)  44.2 us
    another operation x7, other arithmetic, least_squares(): lower_factor = jnp.linalg.cholesky(normal_matrix)  28.8 us
    another operation x12, other arithmetic, orthonormal(): lower_factor = jnp.linalg.cholesky(gram_sum)  26.1 us
    another operation x6, other arithmetic, least_squares(): lax.linalg.triangular_solve(lower_factor, halfway, left_side=True, lower=...  20.1 us
  transfers between devices with their start and end apart: 11, of which 11 were waited for; matrix products, arithmetic and copies ran while one was open for 0% of the time, Pallas kernels for 0%

profile of v1, /device:TPU:1, one launch (start us, length us, event | category | flops | bytes accessed | tf_op | source)
XLA Modules:
  0.0 713.1 jit_solution(17694571819994403369)
XLA Ops:
  6.5 1.7 convert_element_type.12
  8.3 41.9 %all-gather.13.cloned.1.call-done = bf16[8192,64]{0,1:T(8,128)(2,1)} async-done(((bf16[1024,64]{0,1:T(8,128)(2,1)}), bf16[8192,64]{0,1:T(8,128)(2,1)}) %all-gather.13.cloned.1.call-update) | async-done | bytes 1048592 | tf_op jit(solution)/shard_map/all_gather | solution.py:56
  50.2 29.6 %fusion.96 = f32[4096,64]{0,1:T(8,128)} fusion(bf16[4096,8192]{1,0:T(8,128)(2,1)} %param.6, bf16[8192,64]{0,1:T(8,128)(2,1)} %all-gather.13.cloned.1.call-done), kind=kOutput, calls=%fused_computation.159 | convolution fusion | flops 4294967296 | bytes 69206016 | tf_op jit(solution)/shard_map/dot_general | solution.py:52
  79.9 25.2 %reduce-scatter.5.cloned.1.call-done = f32[1024,64]{0,1:T(8,128)} async-done(((f32[4096,64]{0,1:T(8,128)}), f32[1024,64]{0,1:T(8,128)}) %reduce-scatter.5.cloned.1.call-update) | async-done | bytes 262160 | tf_op jit(solution)/shard_map/reduce_scatter | solution.py:57
  105.0 1.4 fusion.92
  106.5 44.2 %all-gather = f32[2048,64]{1,0:T(8,128)S(1)} all-gather(f32[64,64]{1,0:T(8,128)S(1)} %fusion.92), channel_id=2, replica_groups=mesh['row'=8,'col'=4] {'row','col'}, dimensions={0}, use_global_device_ids=true | all-gather | bytes 540672 | tf_op jit(solution)/shard_map/all_gather | solution.py:11
  150.8 5.8 cholesky.195
  156.7 0.6 compare_reduce_fusion.3
  157.4 0.6 select_bitcast_fusion.4
  157.9 4.9 custom-call.25
  162.8 2.0 fusion.93
  165.0 34.3 %all-gather.15.cloned.1.call-done = bf16[8192,64]{0,1:T(8,128)(2,1)} async-done(((bf16[1024,64]{0,1:T(8,128)(2,1)}), bf16[8192,64]{0,1:T(8,128)(2,1)}) %all-gather.15.cloned.1.call-update) | async-done | bytes 1048592 | tf_op jit(solution)/shard_map/all_gather | solution.py:56
  199.2 28.4 %convolution_bitcast_fusion.2 = f32[4096,64]{0,1:T(8,128)} fusion(bf16[8192,64]{0,1:T(8,128)(2,1)} %all-gather.15.cloned.1.call-done, bf16[4096,8192]{1,0:T(8,128)(2,1)} %param.6), kind=kOutput, calls=%fused_computation.2 | convolution fusion | flops 4294967296 | bytes 69206016 | tf_op jit(solution)/shard_map/dot_general | solution.py:52
  227.7 25.2 %reduce-scatter.7.cloned.1.call-done = f32[1024,64]{0,1:T(8,128)} async-done(((f32[4096,64]{0,1:T(8,128)}), f32[1024,64]{0,1:T(8,128)}) %reduce-scatter.7.cloned.1.call-update) | async-done | bytes 262160 | tf_op jit(solution)/shard_map/reduce_scatter | solution.py:57
  252.8 1.0 multiply_add_fusion.2
  253.8 1.3 fusion.12
  255.2 53.3 %all-gather.21.cloned.1.call-done = f32[4096,64]{0,1:T(8,128)} async-done(((f32[128,64]{0,1:T(8,128)}), f32[4096,64]{0,1:T(8,128)}) %all-gather.21.cloned.1.call-update) | async-done | bytes 1048592 | tf_op jit(solution)/shard_map/all_gather | solution.py:11
  308.5 1.4 copy.39
  310.0 0.2 convolution_subtract_fusion.7
  310.3 5.8 cholesky.206
  316.1 0.6 compare_reduce_fusion.2
  316.8 0.7 fusion.73
  317.4 4.9 custom-call.26
  322.3 1.3 convolution_subtract_fusion.1
  323.7 1.1 fusion.94
  324.8 0.2 reduce-scatter.9.cloned.1.call-start
  325.0 37.8 %all-gather.17.cloned.1.call-done = bf16[8192,64]{0,1:T(8,128)(2,1)} async-done(((bf16[1024,64]{0,1:T(8,128)(2,1)}), bf16[8192,64]{0,1:T(8,128)(2,1)}) %all-gather.17.cloned.1.call-update) | async-done | bytes 1048592 | tf_op jit(solution)/shard_map/all_gather | solution.py:56
  362.8 28.4 %convolution_bitcast_fusion.1 = f32[4096,64]{0,1:T(8,128)} fusion(bf16[8192,64]{0,1:T(8,128)(2,1)} %all-gather.17.cloned.1.call-done, bf16[4096,8192]{1,0:T(8,128)(2,1)} %param.6), kind=kOutput, calls=%fused_computation.1 | convolution fusion | flops 4294967296 | bytes 69206016 | tf_op jit(solution)/shard_map/dot_general | solution.py:52
  391.2 25.1 %reduce-scatter.9.cloned.1.call-done = f32[1024,64]{0,1:T(8,128)} async-done(((f32[4096,64]{0,1:T(8,128)}), f32[1024,64]{0,1:T(8,128)}) %reduce-scatter.9.cloned.1.call-update) | async-done | bytes 262160 | tf_op jit(solution)/shard_map/reduce_scatter | solution.py:57
  416.4 1.0 multiply_add_fusion.1
  417.4 1.5 convolution_bitcast_fusion.6
  419.0 57.1 %all-gather.25.cloned.1.call-done = f32[32,192,64]{1,2,0:T(8,128)} async-done(((f32[1,192,64]{1,2,0:T(8,128)}), f32[32,192,64]{1,2,0:T(8,128)}) %all-gather.25.cloned.1.call-update) | async-done | bytes 1572880 | tf_op jit(solution)/shard_map/all_gather | solution.py:11
  476.0 1.7 reduce_sum.38
  478.0 5.8 cholesky.217
  483.9 0.6 compare_reduce_fusion.1
  484.6 0.7 fusion.74
  485.2 4.9 custom-call.27
  490.1 1.4 convolution_subtract_fusion
  491.5 1.1 fusion.95
  492.7 37.1 %all-gather.19.cloned.1.call-done = bf16[8192,64]{0,1:T(8,128)(2,1)} async-done(((bf16[1024,64]{0,1:T(8,128)(2,1)}), bf16[8192,64]{0,1:T(8,128)(2,1)}) %all-gather.19.cloned.1.call-update) | async-done | bytes 1048592 | tf_op jit(solution)/shard_map/all_gather | solution.py:56
  529.8 28.4 %convolution_bitcast_fusion = f32[4096,64]{0,1:T(8,128)} fusion(bf16[8192,64]{0,1:T(8,128)(2,1)} %all-gather.19.cloned.1.call-done, bf16[4096,8192]{1,0:T(8,128)(2,1)} %param.6), kind=kOutput, calls=%fused_computation | convolution fusion | flops 4294967296 | bytes 69206016 | tf_op jit(solution)/shard_map/dot_general | solution.py:52
  558.2 0.3 all-gather.23.cloned.1.call-start
  558.5 24.9 %reduce-scatter.11.cloned.1.call-done = f32[1024,64]{0,1:T(8,128)} async-done(((f32[4096,64]{0,1:T(8,128)}), f32[1024,64]{0,1:T(8,128)}) %reduce-scatter.11.cloned.1.call-update) | async-done | bytes 262160 | tf_op jit(solution)/shard_map/reduce_scatter | solution.py:57
  583.4 1.0 multiply_add_fusion
  584.4 1.7 fusion
  586.2 55.6 %all-gather.23.cloned.1.call-done = f32[8192,64]{0,1:T(8,128)} async-done(((f32[256,64]{0,1:T(8,128)}), f32[8192,64]{0,1:T(8,128)}) %all-gather.23.cloned.1.call-update) | async-done | bytes 2097168 | tf_op jit(solution)/shard_map/all_gather | solution.py:11
  641.7 2.2 copy.40
  643.9 0.2 bitcast_reduce_fusion
  644.2 0.2 convolution_subtract_fusion.5
  644.5 5.8 cholesky.228
  650.3 0.6 compare_reduce_fusion
  651.0 0.7 select_bitcast_fusion.1
  651.7 0.9 fusion.32
  652.6 0.4 fusion.15
  653.2 11.7 %cholesky.77 = f32[128,128]{1,0:T(8,128)S(1)} custom-call(f32[128,128]{1,0:T(8,128)S(1)} %cholesky.237), custom_call_target="Cholesky" | custom-call | tf_op jit(solution)/shard_map/jit(cholesky)/cholesky | solution.py:42
  665.0 9.8 %custom-call.21 = f32[1,128,128]{1,2,0:T(8,128)S(1)} custom-call(f32[1,128,128]{2,1,0:T(8,128)S(1)} %get-tuple-element.28), custom_call_target="InvertDiagBlocksLowerTriangular" | custom-call | tf_op jit(solution)/shard_map/jit(cholesky)/cholesky | solution.py:42
  675.2 5.8 cholesky.135
  681.1 0.7 compare_reduce_fusion.4
  681.8 0.6 compare_reduce_fusion.5
  683.9 19.9 %custom-call.22 = f32[2,128,128]{1,2,0:T(8,128)S(1)} custom-call(f32[2,128,128]{2,1,0:T(8,128)S(1)} %pad_maximum_fusion.7), custom_call_target="InvertDiagBlocksLowerTriangular" | custom-call | tf_op jit(solution)/shard_map/triangular_solve | solution.py:44
  704.3 0.2 fusion.69
  704.5 0.2 fusion.68
  705.0 0.2 fusion.54
  705.2 1.4 convolution_add_fusion
  (60 shorter events, 2.7 us)
Async XLA Ops:
  6.5 98.5 %copy-start = (f32[1024,64]{0,1:T(8,128)S(1)}, f32[1024,64]{0,1:T(8,128)}, u32[]{:S(2)}) copy-start(f32[1024,64]{0,1:T(8,128)} %param.8) | copy-start | bytes 786436
  6.5 98.5 %copy-start.1 = (f32[1024,64]{0,1:T(8,128)S(1)}, f32[1024,64]{0,1:T(8,128)}, u32[]{:S(2)}) copy-start(f32[1024,64]{0,1:T(8,128)} %param.7) | copy-start | bytes 786436
  6.5 43.6 %all-gather.13.cloned.1.call-start = ((), (), s32[]{:S(2)}) async-start(), calls=%async_computation.4 | async-start | bytes 1179648 | tf_op jit(solution)/shard_map/all_gather | solution.py:56
  8.3 96.8 %reduce-scatter.5.cloned.1.call-start = ((), (), s32[]{:S(2)}) async-start(), calls=%async_computation.5 | async-start | bytes 1310720 | tf_op jit(solution)/shard_map/reduce_scatter | solution.py:57
  79.8 119.4 %all-gather.15.cloned.1.call-start = ((), (), s32[]{:S(2)}) async-start(), calls=%async_computation.6 | async-start | bytes 1179648 | tf_op jit(solution)/shard_map/all_gather | solution.py:56
  164.9 87.9 %reduce-scatter.7.cloned.1.call-start = ((), (), s32[]{:S(2)}) async-start(), calls=%async_computation.7 | async-start | bytes 1310720 | tf_op jit(solution)/shard_map/reduce_scatter | solution.py:57
  227.6 80.8 %all-gather.21.cloned.1.call-start = ((), (), s32[]{:S(2)}) async-start(), calls=%async_computation.12 | async-start | bytes 1081344 | tf_op jit(solution)/shard_map/all_gather | solution.py:11
  255.1 107.6 %all-gather.17.cloned.1.call-start = ((), (), s32[]{:S(2)}) async-start(), calls=%async_computation.8 | async-start | bytes 1179648 | tf_op jit(solution)/shard_map/all_gather | solution.py:56
  324.8 91.6 %reduce-scatter.9.cloned.1.call-start = ((), (), s32[]{:S(2)}) async-start(), calls=%async_computation.9 | async-start | bytes 1310720 | tf_op jit(solution)/shard_map/reduce_scatter | solution.py:57
  391.2 84.8 %all-gather.25.cloned.1.call-start = ((), (), s32[]{:S(2)}) async-start(), calls=%async_computation.14 | async-start | bytes 2162688 | tf_op jit(solution)/shard_map/all_gather | solution.py:11
  418.9 110.9 %all-gather.19.cloned.1.call-start = ((), (), s32[]{:S(2)}) async-start(), calls=%async_computation.10 | async-start | bytes 1179648 | tf_op jit(solution)/shard_map/all_gather | solution.py:56
  492.6 90.8 %reduce-scatter.11.cloned.1.call-start = ((), (), s32[]{:S(2)}) async-start(), calls=%async_computation.11 | async-start | bytes 1310720 | tf_op jit(solution)/shard_map/reduce_scatter | solution.py:57
  558.2 83.5 %all-gather.23.cloned.1.call-start = ((), (), s32[]{:S(2)}) async-start(), calls=%async_computation.13 | async-start | bytes 2162688 | tf_op jit(solution)/shard_map/all_gather | solution.py:11
Sparse Core Ops, SparseCore 0:
  9.5 40.6 all-gather.12
  79.9 25.0 reduce-scatter.4
  165.0 34.1 all-gather.14
  227.7 25.0 reduce-scatter.6
  255.6 52.8 all-gather.20
  324.9 37.8 all-gather.16
  391.3 25.0 reduce-scatter.8
  419.2 56.7 all-gather.24
  492.7 37.0 all-gather.18
  558.3 25.0 reduce-scatter.10
  586.3 55.3 all-gather.22
